TPU v7x, 32 devices: a whole 2x2x4 slice. The times are simulated.
32 devices in a mesh: group: 4 (over y, core), row: 2 (over x), col: 4 (over z).
Axes of the slice: x: 2, y: 2, z: 4, core: 2. Of those that a mesh axis runs over, the one named last changes fastest.
Arguments:
- fronts: bfloat16 [8, 12288, 12288], P('group', 'row', 'col'), may hold values from -0.0546875 to 0.0546875
- samples: bfloat16 [256, 8, 12288], P('row', 'group', 'col'), may hold values from -6 to 6
- second_samples: bfloat16 [256, 8, 12288], P('col', 'group', 'row'), may hold values from -6 to 6
- front_sizes: int32 [8], replicated, may hold values from 1536 to 12288, as said below
- parent_ids: int32 [8], replicated, may hold values from 1 to 8, as said below
- block_maps: int32 [8, 2], replicated, may hold values from 0 to 2, as said below
Outputs:
- sampled: bfloat16 [256, 8, 12288], P('col', 'group', 'row')
- projected: bfloat16 [256, 8, 12288], P('row', 'group', 'col')
Inputs may be any that keep to these rules, and one draw needn't show every extreme that they name: `front_sizes`: every front has at least 1536 rows and some front has exactly 12288. `parent_ids`: a front's parent has a larger index; 8 marks a root; the last front is a root. `block_maps`: for a front f with a parent p, entry b with b * 6144 < front_sizes[f] names a parent block q with q * 6144 < front_sizes[p]; all other entries are 2; several child blocks may name one parent block.
All inputs are finite; a program needn't handle non-finite values.
Results may differ from a plain program's by a relative error of at most 0.009.
Values may be sent and summed in bfloat16 or wider, within the bound.
A program may use at most 192 MiB of HBM per device.

v0:
```python
import jax
import jax.numpy as jnp
from jax import lax
from jax.sharding import PartitionSpec as P


def swap_pairs(count):
    return [(0, 1), (1, 0)] if count == 2 else None


def gather_row(value, count, own_row, axis):
    if count != 2:
        return lax.all_gather(value, "row", axis=axis, tiled=True)
    other = lax.ppermute(value, "row", swap_pairs(count))
    first = own_row == 0
    return jnp.concatenate(
        [jnp.where(first, value, other), jnp.where(first, other, value)], axis=axis
    )


def scatter_row(value, count, own_row):
    if count != 2:
        return lax.psum_scatter(
            value.astype(jnp.bfloat16), "row", scatter_dimension=0, tiled=True
        ).astype(jnp.float32)
    half = value.shape[0] // 2
    kept = lax.dynamic_slice_in_dim(value, own_row * half, half, 0)
    sent = lax.dynamic_slice_in_dim(value, (1 - own_row) * half, half, 0).astype(jnp.bfloat16)
    return kept + lax.ppermute(sent, "row", swap_pairs(count)).astype(jnp.float32)


def shards(fronts, samples, second_samples, front_sizes, parent_ids, block_maps):
    local_count, tile_rows, tile_cols = fronts.shape
    row_count = lax.axis_size("row")
    own_group = lax.axis_index("group")
    own_row = lax.axis_index("row")
    own_col = lax.axis_index("col")
    total_fronts = parent_ids.shape[0]
    block_count = block_maps.shape[1]
    own_sizes = lax.dynamic_slice_in_dim(front_sizes, own_group * local_count, local_count, 0)
    row_keep = (own_row * tile_rows + jnp.arange(tile_rows, dtype=jnp.int32))[None, :] < own_sizes[
        :, None
    ]
    col_keep = (own_col * tile_cols + jnp.arange(tile_cols, dtype=jnp.int32))[None, :] < own_sizes[
        :, None
    ]
    own_fronts = own_group * local_count + jnp.arange(local_count, dtype=jnp.int32)
    masked = gather_row(samples, row_count, own_row, 0) * col_keep[None].astype(jnp.bfloat16)
    partial_value = jnp.einsum("sfk,fmk->sfm", masked, fronts, preferred_element_type=jnp.float32)
    partial_value = (partial_value * row_keep[None].astype(jnp.float32)).astype(jnp.bfloat16)
    sampled = lax.psum_scatter(partial_value, "col", scatter_dimension=0, tiled=True)
    portion = lax.all_gather(sampled, ("group", "row"), axis=1, tiled=True)
    number = portion.shape[1]
    source = jnp.arange(number, dtype=jnp.int32)
    front_index = source // (local_count * row_count) * local_count + source % local_count
    block_index = source // local_count % row_count
    front_hot = (front_index[:, None] == jnp.arange(total_fronts, dtype=jnp.int32)[None, :]).astype(
        jnp.int32
    )
    parent = jnp.sum(front_hot * parent_ids[None, :], axis=1)
    map_rows = jnp.sum(front_hot[:, :, None] * block_maps[None, :, :], axis=1)
    block_hot = (jnp.arange(block_count, dtype=jnp.int32)[None, :] == block_index[:, None]).astype(
        jnp.int32
    )
    target = jnp.sum(block_hot * map_rows, axis=1)
    weight = (parent[:, None] == own_fronts[None, :]) & (target[:, None] == own_row)
    extension = jnp.einsum(
        "sik,ij->sjk", portion, weight.astype(jnp.bfloat16), preferred_element_type=jnp.float32
    )
    combined = (second_samples.astype(jnp.float32) + extension).astype(jnp.bfloat16)
    combined = combined * row_keep[None].astype(jnp.bfloat16)
    gathered = lax.all_gather(combined, "col", axis=0, tiled=True)
    product = jnp.einsum("sfm,fmk->sfk", gathered, fronts, preferred_element_type=jnp.float32)
    projected = scatter_row(product, row_count, own_row)
    projected = (projected * col_keep[None].astype(jnp.float32)).astype(jnp.bfloat16)
    return (sampled, projected)


def solution(mesh):
    placed = (
        P("group", "row", "col"),
        P("row", "group", "col"),
        P("col", "group", "row"),
        P(),
        P(),
        P(),
    )
    return jax.shard_map(
        shards,
        mesh=mesh,
        in_specs=placed,
        out_specs=(P("col", "group", "row"), P("row", "group", "col")),
        check_vma=False,
    )
```

profile of v0, /device:TPU:0, one launch (start us, length us, event | category | flops | bytes accessed | tf_op | source)
XLA Modules:
  0.0 491.0 jit_solution(10001149116295977696)
XLA Ops:
  7.2 0.0 reduce-scatter.2.cloned.1.call-start
  7.2 3.0 collective-permute-start
  10.2 0.7 dynamic_slice.9
  11.0 0.1 compare_convert_fusion.2
  11.1 0.1 compare_convert_fusion
  11.2 33.7 %collective-permute-done = bf16[128,2,3072]{2,1,0:T(2,128)(2,1)S(1)} collective-permute-done((bf16[128,2,3072]{2,1,0:T(2,128)(2,1)}, bf16[128,2,3072]{2,1,0:T(2,128)(2,1)S(1)}, u32[]{:S(2)}, u32[]{:S(2)}) %collective-permute-start) | collective-permute-done | bytes 1572896 | tf_op jit(solution)/shard_map/ppermute | solution.py:14
  44.8 1.6 broadcast_select_fusion.1
  46.5 4.6 maximum_multiply_fusion
  51.0 32.3 %fusion.2 = bf16[256,2,6144]{2,0,1:T(8,128)(2,1)} fusion(bf16[2,6144,3072]{2,1,0:T(8,128)(2,1)} %param.6, f32[2,6144]{1,0:T(2,128)S(1)} %get-tuple-element.13, bf16[256,2,3072]{2,1,0:T(2,128)(2,1)S(1)} %maximum_multiply_fusion), kind=kOutput, calls=%fused_computation.3 | convolution fusion | flops 19333644288 | bytes 84983808 | tf_op jit(solution)/shard_map/sfk,fmk->sfm/dot_general | solution.py:49
  83.4 0.0 all-gather.3.cloned.1.call-start
  83.5 112.4 %reduce-scatter.2.cloned.1.call-done = bf16[64,2,6144]{2,0,1:T(8,128)(2,1)} async-done(((bf16[256,2,6144]{2,0,1:T(8,128)(2,1)}), bf16[64,2,6144]{2,0,1:T(8,128)(2,1)}) %reduce-scatter.2.cloned.1.call-update) | async-done | bytes 1572880 | tf_op jit(solution)/shard_map/reduce_scatter | solution.py:51
  195.9 0.2 all-gather.5.cloned.1.call-start
  196.2 0.1 multiply_reduce_fusion
  196.3 0.1 select_reduce_fusion
  196.4 73.9 %all-gather.3.cloned.1.call-done = bf16[64,16,6144]{2,0,1:T(8,128)(2,1)} async-done(((bf16[64,2,6144]{2,0,1:T(8,128)(2,1)}), bf16[64,16,6144]{2,0,1:T(8,128)(2,1)}) %all-gather.3.cloned.1.call-update) | async-done | bytes 12582928 | tf_op jit(solution)/shard_map/all_gather | solution.py:52
  270.3 20.8 %fusion.14 = bf16[64,2,6144]{2,1,0:T(2,128)(2,1)} fusion(bf16[64,16,6144]{2,0,1:T(8,128)(2,1)} %all-gather.3.cloned.1.call-done, bf16[64,2,6144]{2,1,0:T(2,128)(2,1)S(1)} %copy-done.2, bf16[2,6144]{1,0:T(2,128)(2,1)S(1)} %get-tuple-element.12, pred[16]{0:T(512)(128)(4,1)S(1)} %broadcast_compare_fusion, s32[16]{0:T(128)S(1)} %select_reduce_fusion, ...), kind=kOutput, calls=%fused_computation.9 | convolution fusion | flops 28311616 | bytes 15753304 | tf_op jit(solution)/shard_map/sik,ij->sjk/dot_general | solution.py:67
  291.1 115.5 %all-gather.5.cloned.1.call-done = bf16[256,2,6144]{2,1,0:T(2,128)(2,1)} async-done(((bf16[64,2,6144]{2,1,0:T(2,128)(2,1)}), bf16[256,2,6144]{2,1,0:T(2,128)(2,1)}) %all-gather.5.cloned.1.call-update) | async-done | bytes 6291472 | tf_op jit(solution)/shard_map/all_gather | solution.py:72
  406.6 32.8 %fusion.12 = f32[2,256,3072]{2,1,0:T(8,128)} fusion(bf16[2,6144,3072]{2,1,0:T(8,128)(2,1)} %param.6, bf16[256,2,6144]{2,1,0:T(2,128)(2,1)} %all-gather.5.cloned.1.call-done), kind=kOutput, calls=%fused_computation.7 | convolution fusion | flops 19327352832 | bytes 88080384 | tf_op jit(solution)/shard_map/sfm,fmk->sfk/dot_general | solution.py:73
  439.4 3.4 fusion.20
  442.8 1.5 collective-permute-start.1
  444.3 2.8 copy.26
  447.0 32.3 %collective-permute-done.1 = bf16[128,2,3072]{2,0,1:T(8,128)(2,1)S(1)} collective-permute-done((bf16[128,2,3072]{2,0,1:T(8,128)(2,1)}, bf16[128,2,3072]{2,0,1:T(8,128)(2,1)S(1)}, u32[]{:S(2)}, u32[]{:S(2)}) %collective-permute-start.1) | collective-permute-done | bytes 1572896 | tf_op jit(solution)/shard_map/ppermute | solution.py:29
  479.3 2.3 fusion.18
  481.7 2.8 copy.27
  (19 shorter events, 0.1 us)
Async XLA Ops:
  7.2 188.7 %reduce-scatter.2.cloned.1.call-start = ((), (), s32[]{:S(2)}) async-start(), calls=%async_computation.1 | async-start | bytes 7864320 | tf_op jit(solution)/shard_map/reduce_scatter | solution.py:51
  7.2 37.6 %collective-permute-start = (bf16[128,2,3072]{2,1,0:T(2,128)(2,1)}, bf16[128,2,3072]{2,1,0:T(2,128)(2,1)S(1)}, u32[]{:S(2)}, u32[]{:S(2)}) collective-permute-start(bf16[128,2,3072]{2,1,0:T(2,128)(2,1)} %param.7), channel_id=1, source_target_pairs={{0,4},{4,0},{1,5},{5,1},{2,6},{6,2},{3,7},{7,3},{8,12},{12,8},{9,1... | collective-permute-start | bytes 4718600 | tf_op jit(solution)/shard_map/ppermute | solution.py:14
  83.4 112.8 %copy-start.1 = (s32[8,2]{0,1:T(2,128)S(1)}, s32[8,2]{0,1:T(2,128)}, u32[]{:S(2)}) copy-start(s32[8,2]{0,1:T(2,128)} %param.11) | copy-start | bytes 196
  83.4 112.9 %copy-start.3 = (s32[8]{0:T(128)S(1)}, s32[8]{0:T(128)}, u32[]{:S(2)}) copy-start(s32[8]{0:T(128)} %param.10) | copy-start | bytes 100
  83.4 186.9 %copy-start.2 = (bf16[64,2,6144]{2,1,0:T(2,128)(2,1)S(1)}, bf16[64,2,6144]{2,1,0:T(2,128)(2,1)}, u32[]{:S(2)}) copy-start(bf16[64,2,6144]{2,1,0:T(2,128)(2,1)} %param.8) | copy-start | bytes 4718596
  83.4 186.9 %all-gather.3.cloned.1.call-start = ((), (), s32[]{:S(2)}) async-start(), calls=%async_computation.2 | async-start | bytes 14155776 | tf_op jit(solution)/shard_map/all_gather | solution.py:52
  195.9 210.7 %all-gather.5.cloned.1.call-start = ((), (), s32[]{:S(2)}) async-start(), calls=%async_computation.3 | async-start | bytes 7864320 | tf_op jit(solution)/shard_map/all_gather | solution.py:72
  439.4 4.8 copy-start
  442.8 36.5 %collective-permute-start.1 = (bf16[128,2,3072]{2,0,1:T(8,128)(2,1)}, bf16[128,2,3072]{2,0,1:T(8,128)(2,1)S(1)}, u32[]{:S(2)}, u32[]{:S(2)}) collective-permute-start(bf16[128,2,3072]{2,0,1:T(8,128)(2,1)} %fusion.20), channel_id=1, source_target_pairs={{0,4},{4,0},{1,5},{5,1},{2,6},{6,2},{3,7},{7,3},{8,12},{12,8},{9,1... | collective-permute-start | bytes 4718600 | tf_op jit(solution)/shard_map/ppermute | solution.py:29
Sparse Core Ops, SparseCore 0:
  83.5 112.2 reduce-scatter.1
  197.7 72.4 all-gather.2
  291.2 115.3 all-gather.4
where the time goes:
time: 491 us
  waiting for transfers between devices  368 us (75%)
  matrix products  86 us (18%)
  between operations  13.8 us (3%)
  local copies, waits for them, and re-layouts  9.63 us (2%)
  other arithmetic  8.95 us (2%)
    all_gather x1, waiting for transfers between devices, shards(): gathered = lax.all_gather(combined, 'col', axis=0, tiled=True)  115 us
    reduce_scatter x1, waiting for transfers between devices, shards(): lax.psum_scatter(partial_value, 'col', scatter_dimension=0, tiled=True)  112 us
    all_gather x1, waiting for transfers between devices, shards(): portion = lax.all_gather(sampled, ('group', 'row'), axis=1, tiled=True)  73.9 us
    ppermute x1, waiting for transfers between devices, gather_row(): other = lax.ppermute(value, 'row', swap_pairs(count))  33.7 us
    dot_general x1, matrix products, shards(): jnp.einsum('sfm,fmk->sfk', gathered, fronts, preferred_element_type=jnp.f...  32.8 us
    dot_general x1, matrix products, shards(): jnp.einsum('sfk,fmk->sfm', masked, fronts, preferred_element_type=jnp.flo...  32.3 us
    ppermute x1, waiting for transfers between devices, scatter_row(): lax.ppermute(sent, 'row', swap_pairs(count)).astype(jnp.float32)  32.3 us
    dot_general x1, matrix products, shards(): jnp.einsum('sik,ij->sjk', portion, weight.astype(jnp.bfloat16), preferred...  20.8 us
  transfers between devices with their start and end apart: 5, of which 5 were waited for; matrix products, arithmetic and copies ran while one was open for 1% of the time, Pallas kernels for 0%

commit v1 on v0

--- a/solution.py
+++ b/solution.py
@@ -69,7 +69,12 @@
     )
     combined = (second_samples.astype(jnp.float32) + extension).astype(jnp.bfloat16)
     combined = combined * row_keep[None].astype(jnp.bfloat16)
-    gathered = lax.all_gather(combined, "col", axis=0, tiled=True)
+    ring = [combined]
+    for hop in range(3):
+        ring.append(lax.ppermute(ring[-1], "col", [(dev, (dev + 1) % 4) for dev in range(4)]))
+    gathered = jnp.roll(
+        jnp.concatenate(ring[::-1], axis=0), (lax.axis_index("col") + 1) * ring[0].shape[0], axis=0
+    )
     product = jnp.einsum("sfm,fmk->sfk", gathered, fronts, preferred_element_type=jnp.float32)
     projected = scatter_row(product, row_count, own_row)
     projected = (projected * col_keep[None].astype(jnp.float32)).astype(jnp.bfloat16)

time: 491 us -> 520 us (1.059)
  local copies, waits for them, and re-layouts: 9.63 us -> 30.3 us
  matrix products: 86 us -> 94.5 us
  waiting for transfers between devices: 368 us -> 361 us
    all_gather x1 -> x0, waiting for transfers between devices: 115 us -> none  [shards(): gathered = lax.all_gather(combined, 'col', axis=0, tiled=True)]
    ppermute x0 -> x3, waiting for transfers between devices: none -> 111 us  [shards(): lax.ppermute(ring[-1], 'col', [(dev, (dev + 1) % 4) for dev in range(4)])]
    unnamed x10 -> x17, local copies, waits for them, and re-layouts: 5.54 us -> 19.3 us
    dot_general x1, matrix products: 20.8 us -> 29.4 us  [shards(): jnp.einsum('sik,ij->sjk', portion, weight.astype(jnp.bfloat16), preferred...]
    dynamic_slice x0 -> x1, local copies, waits for them, and re-layouts: none -> 5.7 us  [shards(): jnp.roll(jnp.concatenate(ring[::-1], axis=0), (lax.axis_index('col') + 1)...]
  transfers between devices with their start and end apart: 5 -> 7, of which waited for: 5 -> 7; matrix products, arithmetic and copies ran while one was open for 1% -> 1% of each run, Pallas kernels for 0% -> 0%
where the time goes in v1:
time: 520 us; the launch traced here: 516 us
  waiting for transfers between devices  361 us (69%)
  matrix products  94.5 us (18%)
  local copies, waits for them, and re-layouts  30.3 us (6%)
  between operations  14.4 us (3%)
  other arithmetic  8.95 us (2%)
  starting transfers between devices  6.5 us (1%)
    reduce_scatter x1, waiting for transfers between devices, shards(): lax.psum_scatter(partial_value, 'col', scatter_dimension=0, tiled=True)  112 us
    ppermute x3, waiting for transfers between devices, shards(): lax.ppermute(ring[-1], 'col', [(dev, (dev + 1) % 4) for dev in range(4)])  111 us
    all_gather x1, waiting for transfers between devices, shards(): portion = lax.all_gather(sampled, ('group', 'row'), axis=1, tiled=True)  74.2 us
    ppermute x1, waiting for transfers between devices, gather_row(): other = lax.ppermute(value, 'row', swap_pairs(count))  33.7 us
    dot_general x1, matrix products, shards(): jnp.einsum('sfm,fmk->sfk', gathered, fronts, preferred_element_type=jnp.f...  32.8 us
    dot_general x1, matrix products, shards(): jnp.einsum('sfk,fmk->sfm', masked, fronts, preferred_element_type=jnp.flo...  32.3 us
    ppermute x1, waiting for transfers between devices, scatter_row(): lax.ppermute(sent, 'row', swap_pairs(count)).astype(jnp.float32)  30 us
    dot_general x1, matrix products, shards(): jnp.einsum('sik,ij->sjk', portion, weight.astype(jnp.bfloat16), preferred...  29.4 us
  transfers between devices with their start and end apart: 7, of which 7 were waited for; matrix products, arithmetic and copies ran while one was open for 1% of the time, Pallas kernels for 0%

profile of v1, /device:TPU:0, one launch (start us, length us, event | category | flops | bytes accessed | tf_op | source)
XLA Modules:
  0.0 515.9 jit_solution(5050579380346701477)
XLA Ops:
  7.2 3.0 collective-permute-start
  11.2 33.7 %collective-permute-done = bf16[128,2,3072]{2,1,0:T(2,128)(2,1)S(1)} collective-permute-done((bf16[128,2,3072]{2,1,0:T(2,128)(2,1)}, bf16[128,2,3072]{2,1,0:T(2,128)(2,1)S(1)}, u32[]{:S(2)}, u32[]{:S(2)}) %collective-permute-start) | collective-permute-done | bytes 1572896 | tf_op jit(solution)/shard_map/ppermute | solution.py:14
  44.8 1.6 broadcast_select_fusion.1
  46.5 4.6 maximum_multiply_fusion
  51.0 32.3 %fusion.2 = bf16[256,2,6144]{2,0,1:T(8,128)(2,1)} fusion(bf16[2,6144,3072]{2,1,0:T(8,128)(2,1)} %param.6, f32[2,6144]{1,0:T(2,128)S(1)} %get-tuple-element.11, bf16[256,2,3072]{2,1,0:T(2,128)(2,1)S(1)} %maximum_multiply_fusion), kind=kOutput, calls=%fused_computation.3 | convolution fusion | flops 19333644288 | bytes 84983808 | tf_op jit(solution)/shard_map/sfk,fmk->sfm/dot_general | solution.py:49
  83.8 112.0 %reduce-scatter.2.cloned.1.call-done = bf16[64,2,6144]{2,0,1:T(8,128)(2,1)} async-done(((bf16[256,2,6144]{2,0,1:T(8,128)(2,1)}), bf16[64,2,6144]{2,0,1:T(8,128)(2,1)}) %reduce-scatter.2.cloned.1.call-update) | async-done | bytes 1572880 | tf_op jit(solution)/shard_map/reduce_scatter | solution.py:51
  196.1 74.2 %all-gather.2.cloned.1.call-done = bf16[64,16,6144]{2,0,1:T(8,128)(2,1)} async-done(((bf16[64,2,6144]{2,0,1:T(8,128)(2,1)}), bf16[64,16,6144]{2,0,1:T(8,128)(2,1)}) %all-gather.2.cloned.1.call-update) | async-done | bytes 12582928 | tf_op jit(solution)/shard_map/all_gather | solution.py:52
  270.3 29.4 %fusion.14 = bf16[64,2,6144]{2,1,0:T(2,128)(2,1)S(1)} fusion(bf16[64,16,6144]{2,0,1:T(8,128)(2,1)} %all-gather.2.cloned.1.call-done, bf16[64,2,6144]{2,1,0:T(2,128)(2,1)S(1)} %copy-done.2, bf16[2,6144]{1,0:T(2,128)(2,1)S(1)} %get-tuple-element.10, pred[16]{0:T(512)(128)(4,1)S(1)} %broadcast_compare_fusion, s32[16]{0:T(128)S(1)} %select_reduce_fusion, ...), kind=kOutput, calls=%fused_computation.9 | convolution fusion | flops 28311616 | bytes 15753304 | tf_op jit(solution)/shard_map/sik,ij->sjk/dot_general | solution.py:67
  299.7 1.5 collective-permute-start.1
  301.2 36.9 %collective-permute-done.1 = bf16[64,2,6144]{2,1,0:T(2,128)(2,1)S(1)} collective-permute-done((bf16[64,2,6144]{2,1,0:T(2,128)(2,1)S(1)}, bf16[64,2,6144]{2,1,0:T(2,128)(2,1)S(1)}, u32[]{:S(2)}, u32[]{:S(2)}) %collective-permute-start.1) | collective-permute-done | bytes 1572896 | tf_op jit(solution)/shard_map/ppermute | solution.py:74
  338.1 37.6 %collective-permute-done.2 = bf16[64,2,6144]{2,1,0:T(2,128)(2,1)} collective-permute-done((bf16[64,2,6144]{2,1,0:T(2,128)(2,1)S(1)}, bf16[64,2,6144]{2,1,0:T(2,128)(2,1)}, u32[]{:S(2)}, u32[]{:S(2)}) %collective-permute-start.2) | collective-permute-done | bytes 1572896 | tf_op jit(solution)/shard_map/ppermute | solution.py:74
  375.7 36.9 %collective-permute-done.3 = bf16[64,2,6144]{2,1,0:T(2,128)(2,1)} collective-permute-done((bf16[64,2,6144]{2,1,0:T(2,128)(2,1)}, bf16[64,2,6144]{2,1,0:T(2,128)(2,1)}, u32[]{:S(2)}, u32[]{:S(2)}) %collective-permute-start.3) | collective-permute-done | bytes 1572896 | tf_op jit(solution)/shard_map/ppermute | solution.py:74
  412.6 2.5 constant_dynamic-update-slice_fusion.7
  415.1 2.6 constant_dynamic-update-slice_fusion.6
  420.1 2.6 constant_dynamic-update-slice_fusion.3
  422.7 2.6 constant_dynamic-update-slice_fusion.2
  427.6 5.7 %constant_dynamic-slice_fusion = bf16[256,2,6144]{2,1,0:T(2,128)(2,1)} fusion(bf16[512,2,6144]{2,1,0:T(2,128)(2,1)S(1)} %constant_dynamic-update-slice_fusion, s32[]{:T(128)S(6)} %select_n.81), kind=kLoop, calls=%fused_computation.53 | loop fusion | bytes 12582916 | tf_op jit(solution)/shard_map/jit(_roll_dynamic)/dynamic_slice | solution.py:75
  433.3 32.8 %fusion.12 = f32[2,256,3072]{2,1,0:T(8,128)} fusion(bf16[2,6144,3072]{2,1,0:T(8,128)(2,1)} %param.6, bf16[256,2,6144]{2,1,0:T(2,128)(2,1)} %constant_dynamic-slice_fusion), kind=kOutput, calls=%fused_computation.7 | convolution fusion | flops 19327352832 | bytes 88080384 | tf_op jit(solution)/shard_map/sfm,fmk->sfk/dot_general | solution.py:78
  466.1 3.4 fusion.20
  469.5 1.5 collective-permute-start.4
  471.0 2.8 copy.23
  473.7 30.0 %collective-permute-done.4 = bf16[128,2,3072]{2,0,1:T(8,128)(2,1)S(1)} collective-permute-done((bf16[128,2,3072]{2,0,1:T(8,128)(2,1)}, bf16[128,2,3072]{2,0,1:T(8,128)(2,1)S(1)}, u32[]{:S(2)}, u32[]{:S(2)}) %collective-permute-start.4) | collective-permute-done | bytes 1572896 | tf_op jit(solution)/shard_map/ppermute | solution.py:29
  503.7 2.3 fusion.18
  506.0 2.8 copy.24
  (31 shorter events, 6.4 us)
Async XLA Ops:
  7.2 188.7 %reduce-scatter.2.cloned.1.call-start = ((), (), s32[]{:S(2)}) async-start(), calls=%async_computation.1 | async-start | bytes 7864320 | tf_op jit(solution)/shard_map/reduce_scatter | solution.py:51
  7.2 37.6 %collective-permute-start = (bf16[128,2,3072]{2,1,0:T(2,128)(2,1)}, bf16[128,2,3072]{2,1,0:T(2,128)(2,1)S(1)}, u32[]{:S(2)}, u32[]{:S(2)}) collective-permute-start(bf16[128,2,3072]{2,1,0:T(2,128)(2,1)} %param.7), channel_id=1, source_target_pairs={{0,4},{4,0},{1,5},{5,1},{2,6},{6,2},{3,7},{7,3},{8,12},{12,8},{9,1... | collective-permute-start | bytes 4718600 | tf_op jit(solution)/shard_map/ppermute | solution.py:14
  83.4 112.5 %copy-start.1 = (s32[8,2]{0,1:T(2,128)S(1)}, s32[8,2]{0,1:T(2,128)}, u32[]{:S(2)}) copy-start(s32[8,2]{0,1:T(2,128)} %param.11) | copy-start | bytes 196
  83.4 112.6 %copy-start.3 = (s32[8]{0:T(128)S(1)}, s32[8]{0:T(128)}, u32[]{:S(2)}) copy-start(s32[8]{0:T(128)} %param.10) | copy-start | bytes 100
  83.4 186.9 %copy-start.2 = (bf16[64,2,6144]{2,1,0:T(2,128)(2,1)S(1)}, bf16[64,2,6144]{2,1,0:T(2,128)(2,1)}, u32[]{:S(2)}) copy-start(bf16[64,2,6144]{2,1,0:T(2,128)(2,1)} %param.8) | copy-start | bytes 4718596
  83.4 186.9 %all-gather.2.cloned.1.call-start = ((), (), s32[]{:S(2)}) async-start(), calls=%async_computation.2 | async-start | bytes 14155776 | tf_op jit(solution)/shard_map/all_gather | solution.py:52
  299.7 38.4 %collective-permute-start.1 = (bf16[64,2,6144]{2,1,0:T(2,128)(2,1)S(1)}, bf16[64,2,6144]{2,1,0:T(2,128)(2,1)S(1)}, u32[]{:S(2)}, u32[]{:S(2)}) collective-permute-start(bf16[64,2,6144]{2,1,0:T(2,128)(2,1)S(1)} %fusion.14), channel_id=1, source_target_pairs={{0,1},{1,2},{2,3},{3,0},{4,5},{5,6},{6,7},{7,4},{8,9},{9,10},{10,1... | collective-permute-start | bytes 4718600 | tf_op jit(solution)/shard_map/ppermute | solution.py:74
  338.1 37.6 %collective-permute-start.2 = (bf16[64,2,6144]{2,1,0:T(2,128)(2,1)S(1)}, bf16[64,2,6144]{2,1,0:T(2,128)(2,1)}, u32[]{:S(2)}, u32[]{:S(2)}) collective-permute-start(bf16[64,2,6144]{2,1,0:T(2,128)(2,1)S(1)} %collective-permute-done.1), channel_id=1, source_target_pairs={{0,1},{1,2},{2,3},{3,0},{4,5},{5,6},{6,7},{7,4},{8,9},{9,10},{10,1... | collective-permute-start | bytes 4718600 | tf_op jit(solution)/shard_map/ppermute | solution.py:74
  375.7 36.9 %collective-permute-start.3 = (bf16[64,2,6144]{2,1,0:T(2,128)(2,1)}, bf16[64,2,6144]{2,1,0:T(2,128)(2,1)}, u32[]{:S(2)}, u32[]{:S(2)}) collective-permute-start(bf16[64,2,6144]{2,1,0:T(2,128)(2,1)} %collective-permute-done.2), channel_id=1, source_target_pairs={{0,1},{1,2},{2,3},{3,0},{4,5},{5,6},{6,7},{7,4},{8,9},{9,10},{10,1... | collective-permute-start | bytes 4718600 | tf_op jit(solution)/shard_map/ppermute | solution.py:74
  466.1 4.8 copy-start
  469.5 34.2 %collective-permute-start.4 = (bf16[128,2,3072]{2,0,1:T(8,128)(2,1)}, bf16[128,2,3072]{2,0,1:T(8,128)(2,1)S(1)}, u32[]{:S(2)}, u32[]{:S(2)}) collective-permute-start(bf16[128,2,3072]{2,0,1:T(8,128)(2,1)} %fusion.20), channel_id=1, source_target_pairs={{0,4},{4,0},{1,5},{5,1},{2,6},{6,2},{3,7},{7,3},{8,12},{12,8},{9,1... | collective-permute-start | bytes 4718600 | tf_op jit(solution)/shard_map/ppermute | solution.py:29
Sparse Core Ops, SparseCore 0:
  83.5 112.2 reduce-scatter.1
  197.7 72.5 all-gather.1
